TPU v7x, 256 devices: a 4x2x16 block of a 4x16x16 slice. The times are simulated.
256 devices in a mesh: groups: 2 (over y), seq: 16 (over z), head: 8 (over x, core).
Axes of the slice: x: 4, y: 2, z: 16, core: 2. Of those that a mesh axis runs over, the one named last changes fastest.
The devices are a block of a 4x16x16 slice.
Arguments:
- residual: bfloat16 [16384, 2560], P(('groups', 'seq'), 'head'), parts along dimension 0, may hold values from -6 to 6
- x_in: bfloat16 [16384, 5120], P(('groups', 'seq'), 'head'), parts along dimension 0, may hold values from -6 to 6
- bc_in: bfloat16 [16384, 256], P(('groups', 'seq')), parts along dimension 0, may hold values from -1.5 to 1.5
- z_in: bfloat16 [16384, 5120], P(('groups', 'seq'), 'head'), parts along dimension 0, may hold values from -6 to 6
- dt_raw: float32 [80, 16384], P('head', ('groups', 'seq')), parts along dimension 1, may hold values from -5 to 5
- dt_bias: float32 [80], P('head'), may hold values from -3 to 0
- decay_rate: float32 [80], P('head'), may hold values from 0.0003 to 0.15
- d_skip: float32 [80], P('head'), may hold values from 1 to 4
- conv_x_weight: bfloat16 [4, 5120], P(None, 'head'), may hold values from -3 to 3
- conv_x_bias: bfloat16 [5120], P('head'), may hold values from -3 to 3
- conv_bc_weight: bfloat16 [4, 256], replicated, may hold values from -3 to 3
- conv_bc_bias: bfloat16 [256], replicated, may hold values from -3 to 3
- norm_gain: bfloat16 [5120], P('head'), may hold values from 0.5 to 1.5
- out_weight: bfloat16 [5120, 2560], P('head'), may hold values from -0.078125 to 0.078125
- final_gain: bfloat16 [2560], replicated, may hold values from 0.5 to 1.5
- lm_weight: bfloat16 [2560, 25600], P('seq', 'head'), may hold values from -15.811388 to 15.811388
- targets: int32 [16384], P(('groups', 'seq')), parts along dimension 0, may hold values from 0 to 25599
- doc_lengths: int32 [32], P('groups'), parts along dimension 0, may hold values from 1 to 1536, as said below
Outputs:
- block_out: bfloat16 [16384, 2560], P(('groups', 'seq'), 'head'), parts along dimension 0
- doc_loss: float32 [32], P('groups'), parts along dimension 0
There are 2 independent parts, one for each index of `groups`. A program takes and returns all parts, laid end to end along the dimension named above; an argument that names none is the same for every part. Nothing has to cross between parts.
Inputs may be any that keep to these rules, and one draw needn't show every extreme that they name: `doc_lengths`: the lengths of a group's 16 documents, in the order in which they are packed into its 8192 tokens; they sum to 8192.
All inputs are finite; a program needn't handle non-finite values.
Results may differ from a plain program's by a relative error of at most 0.00145.
The roundings to bfloat16 on the way count: a program that leaves them out, or rounds other values in their place, can miss the bound.
Values may be sent and summed in bfloat16 or wider, within the bound.
No kernel may reach another device: no remote copies, remote signals or barrier semaphores. Data moves between devices by JAX's collectives and lax.ppermute only.
A program may use at most 128 MiB of HBM per device.

v0:
```python
import jax
import jax.numpy as jnp
from jax import lax
from jax.sharding import PartitionSpec as P

D = 2560
HEAD_SIZE = 64
STATE = 128
KERNEL = 4
SPAN = 256
INNER = 5120
EPSILON = 1e-05
HIGH = lax.Precision.HIGHEST


def shifted(array, axis, by):
    length = lax.axis_size(axis)
    pairs = [(i, i + by) for i in range(length) if 0 <= i + by < length]
    return lax.ppermute(array, axis, pairs)


def entering(part, axis, combine, identity):
    place = lax.axis_index(axis)
    gathered = jax.tree.map(lambda a: lax.all_gather(a, axis), part)
    state = jax.tree.map(lambda a, e: jnp.zeros_like(a) + jnp.asarray(e, a.dtype), part, identity)

    def one(lap, state):
        return combine(
            state, jax.tree.map(lambda a: lax.dynamic_index_in_dim(a, lap, 0, False), gathered)
        )

    return lax.fori_loop(0, place, one, state)


def cut_along(array, dim, length):
    shape = array.shape
    blocks = array.reshape(*shape[:dim], length, shape[dim] // length, *shape[dim + 1 :])
    return jnp.moveaxis(blocks, dim, 0)


def sent_and_summed(array, axis, dim):
    blocks = cut_along(array, dim, lax.axis_size(axis))
    arrived = lax.all_to_all(blocks, axis, split_axis=0, concat_axis=0, tiled=True)
    return arrived.sum(axis=0)


def joined_along(blocks, dim):
    shape = list(blocks.shape[1:])
    shape[dim] *= blocks.shape[0]
    return jnp.moveaxis(blocks, 0, dim).reshape(shape)


def from_everyone(array, axis):
    length = lax.axis_size(axis)
    return lax.all_to_all(
        jnp.broadcast_to(array[None], (length, *array.shape)), axis, 0, 0, tiled=True
    )


def gather_directly(array, axis, dim):
    return joined_along(from_everyone(array, axis), dim)


def gathered_once(array, axis):
    leaves = jax.tree.leaves(array)
    sequence = sorted(range(len(leaves)), key=lambda k: -leaves[k].size)
    width = (1, *leaves[sequence[0]].shape)[-1]
    lines = [
        jnp.pad(leaves[k].reshape(-1), (0, -leaves[k].size % width)).reshape(-1, width)
        for k in sequence
    ]
    both, at, found = (lax.all_gather(jnp.concatenate(lines), axis), 0, {})
    for k, line in zip(sequence, lines):
        section = both[:, at : at + len(line)].reshape(len(both), -1)
        found[k] = section[:, : leaves[k].size].reshape(-1, *leaves[k].shape)
        at += len(line)
    numbers = iter(range(len(leaves)))
    return jax.tree.map(lambda _: found[next(numbers)], array)


def joined_2(part, axis, combine):
    gathered = gathered_once(part, axis)

    def take(source):
        return jax.tree.map(lambda a: lax.dynamic_index_in_dim(a, source, 0, False), gathered)

    return lax.fori_loop(
        1, lax.axis_size(axis), lambda source, state: combine(state, take(source)), take(0)
    )


def over_copies(array, axis):
    return from_everyone(array, axis).sum(axis=0)


def document_of(positions, doc_lengths):
    starts = jnp.cumsum(doc_lengths) - doc_lengths
    return jnp.sum((positions[:, None] >= starts[None, :]).astype(jnp.int32), axis=1) - 1


def causal_conv(signal, rim_rows, weight, bias, positions, doc_ids, doc_lengths):
    length = signal.shape[0]
    taps = weight.shape[0]
    joined = jnp.concatenate([rim_rows, signal], axis=0).astype(jnp.float32)
    total = jnp.zeros(signal.shape, jnp.float32) + bias.astype(jnp.float32)[None, :]
    for offset in range(taps):
        lag = taps - 1 - offset
        source = document_of(positions - lag, doc_lengths)
        same = (source == doc_ids).astype(jnp.float32)
        total = (
            total
            + weight[offset].astype(jnp.float32)[None, :]
            * joined[offset : offset + length]
            * same[:, None]
        )
    return jax.nn.silu(total).astype(jnp.bfloat16)


def span_step(state, pieces, rates):
    signal, bmat, cmat, steps, doc_ids, doc_prev = pieces
    signal = signal.astype(jnp.float32)
    bmat = bmat.astype(jnp.float32)
    cmat = cmat.astype(jnp.float32)
    climb = jnp.cumsum(steps * rates[:, None], axis=1)
    extent = doc_ids.shape[0]
    order = jnp.arange(extent, dtype=jnp.int32)
    inside = (doc_ids[:, None] == doc_ids[None, :]) & (order[:, None] >= order[None, :])
    gap = climb[:, :, None] - climb[:, None, :]
    decay = jnp.where(inside[None], jnp.exp(-jnp.where(inside[None], gap, 0.0)), 0.0)
    scores = jnp.dot(cmat, bmat.T, precision=HIGH)
    weights = decay * scores[None] * steps[:, None, :]
    output = jnp.einsum("hts,shp->thp", weights, signal, precision=HIGH)
    carried = (doc_ids == doc_prev).astype(jnp.float32)
    entry = jnp.exp(-climb) * carried[None, :]
    output = output + jnp.einsum("tn,hpn->thp", cmat, state, precision=HIGH) * entry.T[:, :, None]
    last = doc_ids[extent - 1]
    tail = (
        jnp.exp(climb - climb[:, extent - 1 :])
        * (doc_ids == last).astype(jnp.float32)[None, :]
        * steps
    )
    kept = jnp.exp(-climb[:, extent - 1]) * (last == doc_prev).astype(jnp.float32)
    fresh = jnp.einsum("hs,shp,sn->hpn", tail, signal, bmat, precision=HIGH)
    return (kept[:, None, None] * state + fresh, output)


def chain_combine(earlier, later):
    return (earlier[0] * later[0], later[0][:, None, None] * earlier[1] + later[1])


def softmax_combine(first_part, second_part):
    peak = jnp.maximum(first_part[0], second_part[0])
    total = first_part[1] * jnp.exp(first_part[0] - peak) + second_part[1] * jnp.exp(
        second_part[0] - peak
    )
    return (peak, total, first_part[2] + second_part[2])


def local(
    residual,
    x_in,
    bc_in,
    z_in,
    dt_raw,
    dt_bias,
    decay_rate,
    d_skip,
    conv_x_weight,
    conv_x_bias,
    conv_bc_weight,
    conv_bc_bias,
    norm_gain,
    out_weight,
    final_gain,
    lm_weight,
    targets,
    doc_lengths,
):
    length = x_in.shape[0]
    inner_here = x_in.shape[1]
    heads_here = dt_raw.shape[0]
    seq_rank = lax.axis_index("seq")
    head_rank = lax.axis_index("head")
    offset_here = seq_rank * length
    positions = offset_here + jnp.arange(length, dtype=jnp.int32)
    doc_ids = document_of(positions, doc_lengths)
    margin = KERNEL - 1
    x_rim, bc_rim = shifted((x_in[length - margin :], bc_in[length - margin :]), "seq", 1)
    signal = causal_conv(x_in, x_rim, conv_x_weight, conv_x_bias, positions, doc_ids, doc_lengths)
    keys_queries = causal_conv(
        bc_in, bc_rim, conv_bc_weight, conv_bc_bias, positions, doc_ids, doc_lengths
    )
    steps = jax.nn.softplus(dt_raw + dt_bias[:, None])
    blocks = length // SPAN
    block_starts = offset_here + jnp.arange(blocks, dtype=jnp.int32) * SPAN
    pieces = (
        signal.reshape(blocks, SPAN, heads_here, HEAD_SIZE),
        keys_queries[:, :STATE].reshape(blocks, SPAN, STATE),
        keys_queries[:, STATE:].reshape(blocks, SPAN, STATE),
        steps.reshape(heads_here, blocks, SPAN).transpose(1, 0, 2),
        doc_ids.reshape(blocks, SPAN),
        document_of(block_starts - 1, doc_lengths),
    )

    def advance(state, piece):
        return span_step(state, piece, decay_rate)

    local_end, outputs = lax.scan(
        advance, jnp.zeros((heads_here, HEAD_SIZE, STATE), jnp.float32), pieces
    )
    outputs = outputs.reshape(length, heads_here, HEAD_SIZE)
    before = document_of(jnp.reshape(offset_here - 1, (1,)), doc_lengths)[0]
    carried = (doc_ids == before).astype(jnp.float32)
    climb = jnp.cumsum(steps * decay_rate[:, None], axis=1)
    through = jnp.exp(-climb[:, length - 1]) * carried[length - 1]
    identity = (jnp.ones_like(through), jnp.zeros_like(local_end))
    incoming = entering((through, local_end), "seq", chain_combine, identity)[1]
    entry = jnp.exp(-climb) * carried[None, :]
    cmat = keys_queries[:, STATE:].astype(jnp.float32)
    outputs = (
        outputs + jnp.einsum("tn,hpn->thp", cmat, incoming, precision=HIGH) * entry.T[:, :, None]
    )
    mixed = outputs + d_skip[None, :, None] * signal.reshape(length, heads_here, HEAD_SIZE).astype(
        jnp.float32
    )
    gated = mixed.reshape(length, inner_here) * jax.nn.silu(z_in.astype(jnp.float32))
    square_sum = lax.psum(jnp.sum(gated * gated, axis=1), "head")
    scale = lax.rsqrt(square_sum / INNER + EPSILON)
    normed = (gated * scale[:, None] * norm_gain.astype(jnp.float32)[None, :]).astype(jnp.bfloat16)
    partial_value = jnp.dot(normed, out_weight, preferred_element_type=jnp.float32)
    share = residual.shape[1]
    projected = sent_and_summed(partial_value, "head", 1)
    block_out = (residual.astype(jnp.float32) + projected).astype(jnp.bfloat16)
    widened = block_out.astype(jnp.float32)
    square_total = lax.psum(jnp.sum(widened * widened, axis=1), "head")
    gain_part = lax.dynamic_slice_in_dim(final_gain, head_rank * share, share, 0)
    final_scale = lax.rsqrt(square_total / D + EPSILON)
    hidden_part = (widened * final_scale[:, None] * gain_part.astype(jnp.float32)[None, :]).astype(
        jnp.bfloat16
    )
    hidden = gather_directly(hidden_part, "head", 1)
    vocab_here = lm_weight.shape[1]
    logits = jnp.dot(
        hidden,
        lax.all_gather(lm_weight, "seq", axis=0, tiled=True),
        preferred_element_type=jnp.float32,
    )
    peak = jnp.max(logits, axis=1)
    total = jnp.sum(jnp.exp(logits - peak[:, None]), axis=1)
    local_target = targets - head_rank * vocab_here
    column = jnp.arange(vocab_here, dtype=jnp.int32)
    picked = jnp.sum(jnp.where(column[None, :] == local_target[:, None], logits, 0.0), axis=1)
    peak_all, total_all, picked_all = joined_2((peak, total, picked), "head", softmax_combine)
    losses = peak_all + jnp.log(total_all) - picked_all
    member = (
        doc_ids[:, None] == jnp.arange(doc_lengths.shape[0], dtype=jnp.int32)[None, :]
    ).astype(jnp.float32)
    sums = over_copies(jnp.dot(losses, member, precision=HIGH), "seq")
    return (block_out, sums / doc_lengths.astype(jnp.float32))


def solution(mesh):
    in_specs = (
        P(("groups", "seq"), "head"),
        P(("groups", "seq"), "head"),
        P(("groups", "seq"), None),
        P(("groups", "seq"), "head"),
        P("head", ("groups", "seq")),
        P("head"),
        P("head"),
        P("head"),
        P(None, "head"),
        P("head"),
        P(),
        P(),
        P("head"),
        P("head", None),
        P(),
        P("seq", "head"),
        P(("groups", "seq")),
        P("groups"),
    )
    out_specs = (P(("groups", "seq"), "head"), P("groups"))
    return jax.shard_map(local, mesh=mesh, in_specs=in_specs, out_specs=out_specs, check_vma=False)
```

profile of v0, /device:TPU:33, one launch (start us, length us, event | category | flops | bytes accessed | tf_op | source)
XLA Modules:
  0.0 454.0 jit_solution(4214907796771070101)
XLA Ops:
  7.3 1.5 slice.103
  8.7 5.8 %collective-permute-start = (bf16[3,640]{1,0:T(4,128)(2,1)}, bf16[3,640]{1,0:T(4,128)(2,1)}, u32[]{:S(2)}, u32[]{:S(2)}) collective-permute-start(bf16[3,640]{1,0:T(4,128)(2,1)} %slice.103), channel_id=1, source_target_pairs={{0,8},{8,16},{16,24},{24,32},{32,40},{40,48},{48,56},{56,64},{64,7... | collective-permute-start | bytes 11528 | tf_op jit(solution)/shard_map/ppermute | solution.py:19
  15.2 3.8 collective-permute-start.1
  23.6 1.5 broadcast_multiply_fusion.1
  25.6 1.5 convert_reduce_fusion.7
  32.7 1.9 multiply_convert_fusion.1
  34.5 2.2 copy.83
  36.7 2.7 reshape.293
  39.4 2.1 copy.85
  41.5 80.0 %while.46 = (s32[]{:T(128)}, f32[10,64,128]{2,1,0:T(8,128)}, f32[2,256,10,64]{1,0,3,2:T(2,128)}, f32[2,10,256]{2,0,1:T(2,128)}, f32[10]{0:T(128)}, /*index=5*/s3...) while((s32[]{:T(128)}, f32[10,64,128]{2,1,0:T(8,128)}, ...), condition=%wide.region_9.10_spmd.clone, body=%wide.region_6.9_spmd.clone.sunk | while | flops 1028866112 | bytes 7581990 | solution.py:208
  43.5 1.9 reduce-window.36
  49.5 1.8 compare_convert_fusion.7
  51.7 4.0 fusion.117
  58.6 1.4 multiply_bitcast_fusion.4
  60.0 1.5 fusion.118
  61.5 1.5 copy.129
  63.0 14.2 %dynamic_update_slice.6 = f32[2,256,10,64]{1,0,3,2:T(2,128)} dynamic-update-slice(f32[2,256,10,64]{1,0,3,2:T(2,128)} %get-tuple-element.624, f32[1,256,10,64]{1,0,3,2:T(1,128)} %copy.129, s32[]{:T(128)} %get-tuple-element.622, s32[]{:T(128)} %constant.152.clone.1..sunk.2, s32[]{:T(128)} %constant.152.clone.1..sunk.2, s32[]{:T(128)} %constant.152.clone.1..sunk.2) | dynamic-update-slice | bytes 1310724 | tf_op jit(solution)/shard_map/while/body/jit(dynamic_update_index_in_dim)/dynamic_update_slice | solution.py:208
  79.2 2.2 convolution_add_fusion.2
  83.4 1.9 reduce-window.36
  89.4 1.8 compare_convert_fusion.7
  91.6 4.0 fusion.117
  98.5 1.4 multiply_bitcast_fusion.4
  99.9 1.6 fusion.118
  101.5 1.5 copy.129
  103.0 14.2 %dynamic_update_slice.6 = f32[2,256,10,64]{1,0,3,2:T(2,128)} dynamic-update-slice(f32[2,256,10,64]{1,0,3,2:T(2,128)} %get-tuple-element.624, f32[1,256,10,64]{1,0,3,2:T(1,128)} %copy.129, s32[]{:T(128)} %get-tuple-element.622, s32[]{:T(128)} %constant.152.clone.1..sunk.2, s32[]{:T(128)} %constant.152.clone.1..sunk.2, s32[]{:T(128)} %constant.152.clone.1..sunk.2) | dynamic-update-slice | bytes 1310724 | tf_op jit(solution)/shard_map/while/body/jit(dynamic_update_index_in_dim)/dynamic_update_slice | solution.py:208
  119.2 2.3 convolution_add_fusion.2
  126.8 39.9 %all-reduce = f32[160]{0:T(256)S(1)} all-reduce(f32[160]{0:T(256)S(1)} %dynamic-update-slice), channel_id=2, replica_groups=mesh['groups'=2,'seq'=16,'head'=8] {'seq'}, use_global_device_ids=true, to_apply=%add | all-reduce | flops 160 | bytes 1280
  167.4 2.4 copy.89
  169.8 3.2 reshape.296
  173.0 32.3 %all-gather.9.cloned.1.call-done = f32[160,64,128]{2,1,0:T(8,128)} async-done(((f32[10,64,128]{2,1,0:T(8,128)}), f32[160,64,128]{2,1,0:T(8,128)}) %all-gather.9.cloned.1.call-update) | async-done | bytes 5242896 | tf_op jit(solution)/shard_map/all_gather | solution.py:24
  207.0 3.7 fusion.46
  210.8 2.8 copy.90
  213.6 2.0 multiply_reduce_fusion
  215.5 20.6 %psum.14 = f32[512]{0:T(512)S(1)} all-reduce(f32[512]{0:T(512)S(1)} %multiply_reduce_fusion), channel_id=1, replica_groups=mesh['groups'=2,'seq'=16,'head'=8] {'head'}, use_global_device_ids=true, to_apply=%region_16.17 | all-reduce | flops 512 | bytes 4096 | tf_op jit(solution)/shard_map/psum | solution.py:227
  236.2 6.4 %fusion.61 = f32[512,2560]{0,1:T(8,128)} fusion(bf16[640,2560]{1,0:T(8,128)(2,1)S(1)} %copy-done, f32[640]{0:T(1024)S(1)} %convert_element_type.158, f32[512]{0:T(512)S(1)} %add_rsqrt_fusion.1, f32[512,640]{1,0:T(8,128)} %copy.90, bf16[512,640]{1,0:T(8,128)(2,1)} %param.27), kind=kOutput, calls=%fused_computation.97 | convolution fusion | flops 1680670720 | bytes 10490368 | tf_op jit(solution)/shard_map/dot_general | solution.py:230
  242.5 5.2 %all-to-all-start = ((f32[8,512,320]{1,2,0:T(8,128)}), f32[8,512,320]{1,2,0:T(8,128)}, u32[]{:S(2)}, u32[]{:S(2)}) async-start(f32[8,512,320]{1,2,0:T(8,128)} %bitcast.151), calls=%async_computation | async-start | bytes 10485760 | tf_op jit(solution)/shard_map/all_to_all | solution.py:43
  248.5 59.3 %all-to-all-done = f32[8,512,320]{1,2,0:T(8,128)} async-done(((f32[8,512,320]{1,2,0:T(8,128)}), f32[8,512,320]{1,2,0:T(8,128)}, u32[]{:S(2)}, u32[]{:S(2)}) %all-to-all-start) | async-done | bytes 5242912 | tf_op jit(solution)/shard_map/all_to_all | solution.py:43
  307.9 4.0 reduce_sum.118
  311.9 2.0 fusion.58
  313.9 13.2 %psum.15 = f32[512]{0:T(512)S(1)} all-reduce(f32[512]{0:T(512)S(1)} %get-tuple-element.424), channel_id=1, replica_groups=mesh['groups'=2,'seq'=16,'head'=8] {'head'}, use_global_device_ids=true, to_apply=%region_19.20 | all-reduce | flops 512 | bytes 4096 | tf_op jit(solution)/shard_map/psum | solution.py:235
  328.2 1.7 broadcast_in_dim.26
  329.9 5.8 %all-to-all-start.1 = ((bf16[8,512,320]{1,2,0:T(8,128)(2,1)}), bf16[8,512,320]{1,2,0:T(8,128)(2,1)}, u32[]{:S(2)}, u32[]{:S(2)}) async-start(bf16[8,512,320]{1,2,0:T(8,128)(2,1)} %broadcast_in_dim.26), calls=%async_computation.1 | async-start | bytes 5242880 | tf_op jit(solution)/shard_map/all_to_all | solution.py:55
  335.7 32.0 %all-to-all-done.1 = bf16[8,512,320]{1,2,0:T(8,128)(2,1)} async-done(((bf16[8,512,320]{1,2,0:T(8,128)(2,1)}), bf16[8,512,320]{1,2,0:T(8,128)(2,1)}, u32[]{:S(2)}, u32[]{:S(2)}) %all-to-all-start.1) | async-done | bytes 2621472 | tf_op jit(solution)/shard_map/all_to_all | solution.py:55
  367.7 27.6 %all-gather.7.cloned.1.call-done = bf16[2560,3200]{1,0:T(8,128)(2,1)} async-done(((bf16[160,3200]{1,0:T(8,128)(2,1)}), bf16[2560,3200]{1,0:T(8,128)(2,1)}) %all-gather.7.cloned.1.call-update) | async-done | bytes 16384016 | tf_op jit(solution)/shard_map/all_gather | solution.py:245
  395.3 14.5 %fusion.89 = (f32[512]{0:T(512)S(1)}, f32[512,3200]{1,0:T(8,128)S(1)}) fusion(bf16[512,2560]{0,1:T(8,128)(2,1)} %bitcast.23, bf16[2560,3200]{1,0:T(8,128)(2,1)} %all-gather.7.cloned.1.call-done), kind=kOutput, calls=%fused_computation.170 | convolution fusion | flops 8390245888 | bytes 25561088 | tf_op jit(solution)/shard_map/dot_general | solution.py:243
  409.8 2.0 exponential_reduce_fusion
  411.8 13.9 %all-gather.3 = f32[8,3,512]{2,1,0:T(4,128)S(1)} all-gather(f32[1,3,512]{2,1,0:T(4,128)S(1)} %maximum_bitcast_fusion), channel_id=4, replica_groups=mesh['groups'=2,'seq'=16,'head'=8] {'head'}, dimensions={0}, use_global_device_ids=true | all-gather | bytes 55296 | tf_op jit(solution)/shard_map/all_gather | solution.py:72
  426.8 19.8 %all_to_all.16 = f32[16,1,16]{2,1,0:T(1,128)S(1)} all-to-all(f32[16,1,16]{2,1,0:T(1,128)S(1)} %broadcast_in_dim.28), channel_id=1, replica_groups=mesh['groups'=2,'seq'=16,'head'=8] {'seq'}, dimensions={0} | all-to-all | bytes 2048 | tf_op jit(solution)/shard_map/all_to_all | solution.py:55
  (177 shorter events, 41.2 us)
Async XLA Ops:
  7.2 229.0 %copy-start = (bf16[640,2560]{1,0:T(8,128)(2,1)S(1)}, bf16[640,2560]{1,0:T(8,128)(2,1)}, u32[]{:S(2)}) copy-start(bf16[640,2560]{1,0:T(8,128)(2,1)} %param.37) | copy-start | bytes 9830404
  7.2 198.1 %all-gather.9.cloned.1.call-start = ((), (), s32[]{:S(2)}) async-start(), calls=%async_computation.4 | async-start | bytes 5570560 | tf_op jit(solution)/shard_map/all_gather | solution.py:24
  8.7 23.1 %collective-permute-start = (bf16[3,640]{1,0:T(4,128)(2,1)}, bf16[3,640]{1,0:T(4,128)(2,1)}, u32[]{:S(2)}, u32[]{:S(2)}) collective-permute-start(bf16[3,640]{1,0:T(4,128)(2,1)} %slice.103), channel_id=1, source_target_pairs={{0,8},{8,16},{16,24},{24,32},{32,40},{40,48},{48,56},{56,64},{64,7... | collective-permute-start | bytes 11528 | tf_op jit(solution)/shard_map/ppermute | solution.py:19
  15.2 14.4 %collective-permute-start.1 = (bf16[3,256]{1,0:T(4,128)(2,1)S(1)}, bf16[3,256]{1,0:T(4,128)(2,1)S(1)}, u32[]{:S(2)}, u32[]{:S(2)}) collective-permute-start(bf16[3,256]{1,0:T(4,128)(2,1)S(1)} %slice.112), channel_id=1, source_target_pairs={{0,8},{8,16},{16,24},{24,32},{32,40},{40,48},{48,56},{56,64},{64,7... | collective-permute-start | bytes 4616 | tf_op jit(solution)/shard_map/ppermute | solution.py:19
  22.9 7.7 %copy-start.13 = (s32[512]{0:T(512)}, s32[512]{0:T(512)S(1)}, u32[]{:S(2)}) copy-start(s32[512]{0:T(512)S(1)} %broadcast_add_fusion.2) | copy-start | bytes 6148
  30.7 1.1 copy-start.5
  31.1 0.7 copy-start.3
  31.1 1.5 copy-start.8
  31.1 1.5 copy-start.9
  31.1 1.5 copy-start.10
  31.1 1.5 copy-start.11
  48.3 3.4 copy-start.1
  58.6 1.4 copy-start.7
  61.5 17.7 %copy-start.2 = (f32[256,10]{0,1:T(8,128)S(1)}, f32[256,10]{0,1:T(8,128)}, u32[]{:S(2)}) copy-start(f32[256,10]{0,1:T(8,128)} %get-tuple-element.606) | copy-start | bytes 30724 | tf_op jit(solution)/shard_map/while
  88.1 3.4 copy-start.1
  98.5 1.4 copy-start.7
  101.5 17.7 %copy-start.2 = (f32[256,10]{0,1:T(8,128)S(1)}, f32[256,10]{0,1:T(8,128)}, u32[]{:S(2)}) copy-start(f32[256,10]{0,1:T(8,128)} %get-tuple-element.606) | copy-start | bytes 30724 | tf_op jit(solution)/shard_map/while
  121.4 0.9 copy-start.12
  121.4 1.5 copy-start.6
  121.4 3.0 copy-start.19
  121.4 45.3 %copy-start.15 = (bf16[640]{0:T(1024)(128)(2,1)S(1)}, bf16[640]{0:T(1024)(128)(2,1)}, u32[]{:S(2)}) copy-start(bf16[640]{0:T(1024)(128)(2,1)} %param.36) | copy-start | bytes 3844
  121.5 273.8 %all-gather.7.cloned.1.call-start = ((), (), s32[]{:S(2)}) async-start(), calls=%async_computation.3 | async-start | bytes 17408000 | tf_op jit(solution)/shard_map/all_gather | solution.py:245
  206.1 0.9 copy-start.4
  206.1 1.0 copy-start.18
  242.5 65.3 %all-to-all-start = ((f32[8,512,320]{1,2,0:T(8,128)}), f32[8,512,320]{1,2,0:T(8,128)}, u32[]{:S(2)}, u32[]{:S(2)}) async-start(f32[8,512,320]{1,2,0:T(8,128)} %bitcast.151), calls=%async_computation | async-start | bytes 10485760 | tf_op jit(solution)/shard_map/all_to_all | solution.py:43
  329.9 5.8 %copy-start.17 = (s32[512]{0:T(512)S(1)}, s32[512]{0:T(512)}, u32[]{:S(2)}) copy-start(s32[512]{0:T(512)} %param.40) | copy-start | bytes 6148
  329.9 37.8 %all-to-all-start.1 = ((bf16[8,512,320]{1,2,0:T(8,128)(2,1)}), bf16[8,512,320]{1,2,0:T(8,128)(2,1)}, u32[]{:S(2)}, u32[]{:S(2)}) async-start(bf16[8,512,320]{1,2,0:T(8,128)(2,1)} %broadcast_in_dim.26), calls=%async_computation.1 | async-start | bytes 5242880 | tf_op jit(solution)/shard_map/all_to_all | solution.py:55
  409.8 16.7 %copy-start.14 = (s32[512]{0:T(512)S(1)}, s32[512]{0:T(512)}, u32[]{:S(2)}) copy-start(s32[512]{0:T(512)} %copy-done.13) | copy-start | bytes 6148
  409.8 36.8 %copy-start.16 = (s32[16]{0:T(128)S(1)}, s32[16]{0:T(128)}, u32[]{:S(2)}) copy-start(s32[16]{0:T(128)} %param.41) | copy-start | bytes 196
Sparse Core Ops, SparseCore 0:
  121.6 83.6 all-gather.8
  207.1 188.1 all-gather.6
where the time goes:
time: 458 us; the launch traced here: 454 us
  waiting for transfers between devices  152 us (33%)
  blocking collectives  107 us (23%)
  local copies, waits for them, and re-layouts  69.2 us (15%)
  other arithmetic  44.6 us (10%)
  matrix products  40.9 us (9%)
  starting transfers between devices  20.8 us (5%)
  between operations  15.8 us (3%)
    all_to_all x1, waiting for transfers between devices, sent_and_summed(): lax.all_to_all(blocks, axis, split_axis=0, concat_axis=0, tiled=True)  59.3 us
    unnamed x1, blocking collectives  39.9 us
    all_gather x1, waiting for transfers between devices, entering(): gathered = jax.tree.map(lambda a: lax.all_gather(a, axis), part)  32.3 us
    all_to_all x1, waiting for transfers between devices, from_everyone(): lax.all_to_all(jnp.broadcast_to(array[None], (length, *array.shape)), axi...  32 us
    dynamic_update_slice x4, local copies, waits for them, and re-layouts, local(): lax.scan(advance, jnp.zeros((heads_here, HEAD_SIZE, STATE), jnp.float32),...  31.3 us
    all_gather x1, waiting for transfers between devices, local(): lax.all_gather(lm_weight, 'seq', axis=0, tiled=True)  27.6 us
    psum x1, blocking collectives, local(): square_sum = lax.psum(jnp.sum(gated * gated, axis=1), 'head')  20.6 us
    all_to_all x1, blocking collectives, from_everyone(): lax.all_to_all(jnp.broadcast_to(array[None], (length, *array.shape)), axi...  19.8 us
  transfers between devices with their start and end apart: 6, of which 4 were waited for; matrix products, arithmetic and copies ran while one was open for 10% of the time, Pallas kernels for 0%

commit v1 on v0

--- a/solution.py
+++ b/solution.py
@@ -11,6 +11,12 @@
 INNER = 5120
 EPSILON = 1e-05
 HIGH = lax.Precision.HIGHEST
+
+
+def gather_from_all(x, axis, dim):
+    peers = lax.axis_size(axis)
+    repeats = [peers if d == dim else 1 for d in range(x.ndim)]
+    return lax.all_to_all(jnp.tile(x, repeats), axis, split_axis=dim, concat_axis=dim, tiled=True)
 
 
 def shifted(array, axis, by):
@@ -241,9 +247,7 @@
     hidden = gather_directly(hidden_part, "head", 1)
     vocab_here = lm_weight.shape[1]
     logits = jnp.dot(
-        hidden,
-        lax.all_gather(lm_weight, "seq", axis=0, tiled=True),
-        preferred_element_type=jnp.float32,
+        hidden, gather_from_all(lm_weight, "seq", 0), preferred_element_type=jnp.float32
     )
     peak = jnp.max(logits, axis=1)
     total = jnp.sum(jnp.exp(logits - peak[:, None]), axis=1)

time: 458 us -> 1170 us (2.55)
  waiting for transfers between devices: 152 us -> 794 us
  blocking collectives: 107 us -> 144 us
  starting transfers between devices: 20.8 us -> 46.1 us
    all_to_all x1, waiting for transfers between devices: 32 us -> 704 us  [gather_from_all(): lax.all_to_all(jnp.tile(x, repeats), axis, split_axis=dim, concat_axis=di...]
    all_to_all x1 -> x2, blocking collectives: 19.8 us -> 57.9 us  [from_everyone(): lax.all_to_all(jnp.broadcast_to(array[None], (length, *array.shape)), axi...]
    all_gather x1 -> x0, waiting for transfers between devices: 27.6 us -> none  [local(): lax.all_gather(lm_weight, 'seq', axis=0, tiled=True)]
    all_to_all x1, starting transfers between devices: 5.77 us -> 31.3 us  [gather_from_all(): lax.all_to_all(jnp.tile(x, repeats), axis, split_axis=dim, concat_axis=di...]
  transfers between devices with their start and end apart: 6 -> 5, of which waited for: 4 -> 3; matrix products, arithmetic and copies ran while one was open for 10% -> 2% of each run, Pallas kernels for 0% -> 0%
where the time goes in v1:
time: 1170 us; the launch traced here: 1160 us
  waiting for transfers between devices  794 us (68%)
  blocking collectives  144 us (12%)
  local copies, waits for them, and re-layouts  76 us (6%)
  starting transfers between devices  46.1 us (4%)
  other arithmetic  42.6 us (4%)
  matrix products  40.1 us (3%)
  between operations  15.8 us (1%)
    all_to_all x1, waiting for transfers between devices, gather_from_all(): lax.all_to_all(jnp.tile(x, repeats), axis, split_axis=dim, concat_axis=di...  704 us
    all_to_all x1, waiting for transfers between devices, sent_and_summed(): lax.all_to_all(blocks, axis, split_axis=0, concat_axis=0, tiled=True)  59.3 us
    all_to_all x2, blocking collectives, from_everyone(): lax.all_to_all(jnp.broadcast_to(array[None], (length, *array.shape)), axi...  57.9 us
    unnamed x1, blocking collectives  39.5 us
    dynamic_update_slice x4, local copies, waits for them, and re-layouts, local(): lax.scan(advance, jnp.zeros((heads_here, HEAD_SIZE, STATE), jnp.float32),...  31.3 us
    all_to_all x1, starting transfers between devices, gather_from_all(): lax.all_to_all(jnp.tile(x, repeats), axis, split_axis=dim, concat_axis=di...  31.3 us
    all_gather x1, waiting for transfers between devices, entering(): gathered = jax.tree.map(lambda a: lax.all_gather(a, axis), part)  30.4 us
  transfers between devices with their start and end apart: 5, of which 3 were waited for; matrix products, arithmetic and copies ran while one was open for 2% of the time, Pallas kernels for 0%

profile of v1, /device:TPU:33, one launch (start us, length us, event | category | flops | bytes accessed | tf_op | source)
XLA Modules:
  0.0 1161.7 jit_solution(10600358815875827660)
XLA Ops:
  7.3 1.5 slice.103
  8.7 5.8 collective-permute-start
  15.2 3.8 collective-permute-start.1
  23.7 1.4 broadcast_multiply_fusion.1
  25.7 1.5 convert_reduce_fusion.7
  32.8 1.9 multiply_convert_fusion.1
  34.7 2.2 copy.83
  36.9 2.7 reshape.300
  39.5 2.0 copy.85
  41.6 80.2 %while.46 = (s32[]{:T(128)}, f32[10,64,128]{2,1,0:T(8,128)}, f32[2,256,10,64]{1,0,3,2:T(2,128)}, f32[2,10,256]{2,0,1:T(2,128)}, f32[10]{0:T(128)}, /*index=5*/s3...) while((s32[]{:T(128)}, f32[10,64,128]{2,1,0:T(8,128)}, ...), condition=%wide.region_9.10_spmd.clone, body=%wide.region_6.9_spmd.clone.sunk | while | flops 1028866112 | bytes 7581990 | solution.py:214
  43.6 1.9 reduce-window.36
  45.5 1.5 slice_reduce_fusion.5
  49.8 1.9 compare_convert_fusion.7
  52.1 4.0 fusion.117
  58.9 1.4 multiply_bitcast_fusion.4
  60.3 1.5 fusion.118
  61.8 1.5 copy.129
  63.3 14.2 %dynamic_update_slice.6 = f32[2,256,10,64]{1,0,3,2:T(2,128)} dynamic-update-slice(f32[2,256,10,64]{1,0,3,2:T(2,128)} %get-tuple-element.624, f32[1,256,10,64]{1,0,3,2:T(1,128)} %copy.129, s32[]{:T(128)} %get-tuple-element.622, s32[]{:T(128)} %constant.152.clone.1..sunk.2, s32[]{:T(128)} %constant.152.clone.1..sunk.2, s32[]{:T(128)} %constant.152.clone.1..sunk.2) | dynamic-update-slice | bytes 1310724 | tf_op jit(solution)/shard_map/while/body/jit(dynamic_update_index_in_dim)/dynamic_update_slice | solution.py:214
  79.4 2.2 convolution_add_fusion.2
  83.6 1.9 reduce-window.36
  85.5 1.5 slice_reduce_fusion.5
  89.8 1.9 compare_convert_fusion.7
  92.1 4.0 fusion.117
  100.3 1.6 fusion.118
  101.9 1.5 copy.129
  103.4 14.2 %dynamic_update_slice.6 = f32[2,256,10,64]{1,0,3,2:T(2,128)} dynamic-update-slice(f32[2,256,10,64]{1,0,3,2:T(2,128)} %get-tuple-element.624, f32[1,256,10,64]{1,0,3,2:T(1,128)} %copy.129, s32[]{:T(128)} %get-tuple-element.622, s32[]{:T(128)} %constant.152.clone.1..sunk.2, s32[]{:T(128)} %constant.152.clone.1..sunk.2, s32[]{:T(128)} %constant.152.clone.1..sunk.2) | dynamic-update-slice | bytes 1310724 | tf_op jit(solution)/shard_map/while/body/jit(dynamic_update_index_in_dim)/dynamic_update_slice | solution.py:214
  119.5 2.3 convolution_add_fusion.2
  128.4 39.5 %all-reduce = f32[160]{0:T(256)S(1)} all-reduce(f32[160]{0:T(256)S(1)} %dynamic-update-slice), channel_id=2, replica_groups=mesh['groups'=2,'seq'=16,'head'=8] {'seq'}, use_global_device_ids=true, to_apply=%add | all-reduce | flops 160 | bytes 1280
  170.0 2.4 copy.89
  172.4 3.3 reshape.303
  175.7 30.4 %all-gather.6.cloned.1.call-done = f32[160,64,128]{2,1,0:T(8,128)} async-done(((f32[10,64,128]{2,1,0:T(8,128)}), f32[160,64,128]{2,1,0:T(8,128)}) %all-gather.6.cloned.1.call-update) | async-done | bytes 5242896 | tf_op jit(solution)/shard_map/all_gather | solution.py:30
  207.8 3.8 fusion.46
  211.6 2.8 copy.90
  214.4 2.0 multiply_reduce_fusion
  216.4 19.8 %psum.14 = f32[512]{0:T(512)S(1)} all-reduce(f32[512]{0:T(512)S(1)} %multiply_reduce_fusion), channel_id=1, replica_groups=mesh['groups'=2,'seq'=16,'head'=8] {'head'}, use_global_device_ids=true, to_apply=%region_16.17 | all-reduce | flops 512 | bytes 4096 | tf_op jit(solution)/shard_map/psum | solution.py:233
  236.2 6.3 fusion.61
  242.5 5.0 all-to-all-start
  248.4 59.3 %all-to-all-done = f32[8,512,320]{1,2,0:T(8,128)} async-done(((f32[8,512,320]{1,2,0:T(8,128)}), f32[8,512,320]{1,2,0:T(8,128)}, u32[]{:S(2)}, u32[]{:S(2)}) %all-to-all-start) | async-done | bytes 5242912 | tf_op jit(solution)/shard_map/all_to_all | solution.py:49
  307.7 3.2 reduce_sum.118
  311.0 12.8 %psum.15 = f32[512]{0:T(512)S(1)} all-reduce(f32[512]{0:T(512)S(1)} %get-tuple-element.424), channel_id=1, replica_groups=mesh['groups'=2,'seq'=16,'head'=8] {'head'}, use_global_device_ids=true, to_apply=%region_19.20 | all-reduce | flops 512 | bytes 4096 | tf_op jit(solution)/shard_map/psum | solution.py:241
  324.2 36.1 %all_to_all.25 = bf16[8,512,320]{1,2,0:T(8,128)(2,1)} all-to-all(bf16[8,512,320]{1,2,0:T(8,128)(2,1)S(1)} %broadcast_in_dim.26), channel_id=1, replica_groups=mesh['groups'=2,'seq'=16,'head'=8] {'head'}, dimensions={0} | all-to-all | bytes 5242880 | tf_op jit(solution)/shard_map/all_to_all | solution.py:61
  360.3 5.8 tile.2
  366.1 31.3 %all-to-all-start.2 = ((bf16[16,160,3200]{2,1,0:T(8,128)(2,1)}), bf16[16,160,3200]{2,1,0:T(8,128)(2,1)}, u32[]{:S(2)}, u32[]{:S(2)}) async-start(bf16[16,160,3200]{2,1,0:T(8,128)(2,1)} %tile.2), calls=%async_computation.2 | async-start | bytes 32768000 | tf_op jit(solution)/shard_map/all_to_all | solution.py:19
  397.4 704.2 %all-to-all-done.2 = bf16[16,160,3200]{2,1,0:T(8,128)(2,1)} async-done(((bf16[16,160,3200]{2,1,0:T(8,128)(2,1)}), bf16[16,160,3200]{2,1,0:T(8,128)(2,1)}, u32[]{:S(2)}, u32[]{:S(2)}) %all-to-all-start.2) | async-done | bytes 16384032 | tf_op jit(solution)/shard_map/all_to_all | solution.py:19
  1101.5 13.8 %fusion.89 = (f32[512]{0:T(512)S(1)}, f32[512,3200]{1,0:T(8,128)S(1)}) fusion(bf16[512,2560]{0,1:T(8,128)(2,1)S(1)} %bitcast.158, bf16[2560,3200]{1,0:T(8,128)(2,1)} %bitcast.24), kind=kOutput, calls=%fused_computation.170 | convolution fusion | flops 8390245888 | bytes 25561088 | tf_op jit(solution)/shard_map/dot_general | solution.py:249
  1115.4 2.0 exponential_reduce_fusion
  1117.4 14.2 %all-gather.3 = f32[8,3,512]{2,1,0:T(4,128)S(1)} all-gather(f32[1,3,512]{2,1,0:T(4,128)S(1)} %maximum_bitcast_fusion), channel_id=4, replica_groups=mesh['groups'=2,'seq'=16,'head'=8] {'head'}, dimensions={0}, use_global_device_ids=true | all-gather | bytes 55296 | tf_op jit(solution)/shard_map/all_gather | solution.py:78
  1132.6 21.8 %all_to_all.26 = f32[16,1,16]{2,1,0:T(1,128)S(1)} all-to-all(f32[16,1,16]{2,1,0:T(1,128)S(1)} %broadcast_in_dim.28), channel_id=1, replica_groups=mesh['groups'=2,'seq'=16,'head'=8] {'seq'}, dimensions={0} | all-to-all | bytes 2048 | tf_op jit(solution)/shard_map/all_to_all | solution.py:61
  (178 shorter events, 42.2 us)
Async XLA Ops:
  7.2 229.1 %copy-start = (bf16[640,2560]{1,0:T(8,128)(2,1)S(1)}, bf16[640,2560]{1,0:T(8,128)(2,1)}, u32[]{:S(2)}) copy-start(bf16[640,2560]{1,0:T(8,128)(2,1)} %param.37) | copy-start | bytes 9830404
  7.2 198.9 %all-gather.6.cloned.1.call-start = ((), (), s32[]{:S(2)}) async-start(), calls=%async_computation.4 | async-start | bytes 5570560 | tf_op jit(solution)/shard_map/all_gather | solution.py:30
  8.7 23.2 %collective-permute-start = (bf16[3,640]{1,0:T(4,128)(2,1)}, bf16[3,640]{1,0:T(4,128)(2,1)}, u32[]{:S(2)}, u32[]{:S(2)}) collective-permute-start(bf16[3,640]{1,0:T(4,128)(2,1)} %slice.103), channel_id=1, source_target_pairs={{0,8},{8,16},{16,24},{24,32},{32,40},{40,48},{48,56},{56,64},{64,7... | collective-permute-start | bytes 11528 | tf_op jit(solution)/shard_map/ppermute | solution.py:25
  15.2 14.5 %collective-permute-start.1 = (bf16[3,256]{1,0:T(4,128)(2,1)S(1)}, bf16[3,256]{1,0:T(4,128)(2,1)S(1)}, u32[]{:S(2)}, u32[]{:S(2)}) collective-permute-start(bf16[3,256]{1,0:T(4,128)(2,1)S(1)} %slice.112), channel_id=1, source_target_pairs={{0,8},{8,16},{16,24},{24,32},{32,40},{40,48},{48,56},{56,64},{64,7... | collective-permute-start | bytes 4616 | tf_op jit(solution)/shard_map/ppermute | solution.py:25
  22.9 7.8 copy-start.16
  30.7 1.2 copy-start.9
  31.2 0.7 copy-start.5
  31.2 1.5 copy-start.12
  31.2 1.5 copy-start.13
  31.2 1.5 copy-start.14
  31.2 1.5 copy-start.15
  48.5 3.6 copy-start.3
  58.9 1.4 copy-start.11
  61.8 17.6 %copy-start.4 = (f32[256,10]{0,1:T(8,128)S(1)}, f32[256,10]{0,1:T(8,128)}, u32[]{:S(2)}) copy-start(f32[256,10]{0,1:T(8,128)} %get-tuple-element.606) | copy-start | bytes 30724 | tf_op jit(solution)/shard_map/while
  88.5 3.6 copy-start.3
  98.9 1.4 copy-start.11
  101.9 17.6 %copy-start.4 = (f32[256,10]{0,1:T(8,128)S(1)}, f32[256,10]{0,1:T(8,128)}, u32[]{:S(2)}) copy-start(f32[256,10]{0,1:T(8,128)} %get-tuple-element.606) | copy-start | bytes 30724 | tf_op jit(solution)/shard_map/while
  206.9 0.9 copy-start.6
  206.9 1.0 copy-start.20
  242.5 65.2 %all-to-all-start = ((f32[8,512,320]{1,2,0:T(8,128)}), f32[8,512,320]{1,2,0:T(8,128)}, u32[]{:S(2)}, u32[]{:S(2)}) async-start(f32[8,512,320]{1,2,0:T(8,128)} %bitcast.152), calls=%async_computation | async-start | bytes 10485760 | tf_op jit(solution)/shard_map/all_to_all | solution.py:49
  248.3 62.5 %copy-start.10 = (bf16[512,320]{0,1:T(8,128)(2,1)S(1)}, bf16[512,320]{0,1:T(8,128)(2,1)}, u32[]{:S(2)}) copy-start(bf16[512,320]{0,1:T(8,128)(2,1)} %param.24) | copy-start | bytes 983044
  311.0 12.8 %copy-start.7 = (bf16[512,320]{0,1:T(8,128)(2,1)}, bf16[512,320]{0,1:T(8,128)(2,1)S(1)}, u32[]{:S(2)}) copy-start(bf16[512,320]{0,1:T(8,128)(2,1)S(1)} %get-tuple-element.425) | copy-start | bytes 983044
  324.2 36.1 %copy-start.8 = (bf16[160,3200]{1,0:T(8,128)(2,1)S(1)}, bf16[160,3200]{1,0:T(8,128)(2,1)}, u32[]{:S(2)}) copy-start(bf16[160,3200]{1,0:T(8,128)(2,1)} %param.39) | copy-start | bytes 3072004
  366.1 31.3 %copy-start.19 = (s32[512]{0:T(512)S(1)}, s32[512]{0:T(512)}, u32[]{:S(2)}) copy-start(s32[512]{0:T(512)} %param.40) | copy-start | bytes 6148
  366.1 735.5 %copy-start.2 = (bf16[8,512,320]{1,2,0:T(8,128)(2,1)S(1)}, bf16[8,512,320]{1,2,0:T(8,128)(2,1)}, u32[]{:S(2)}) copy-start(bf16[8,512,320]{1,2,0:T(8,128)(2,1)} %all_to_all.25) | copy-start | bytes 7864324
  366.1 735.5 %all-to-all-start.2 = ((bf16[16,160,3200]{2,1,0:T(8,128)(2,1)}), bf16[16,160,3200]{2,1,0:T(8,128)(2,1)}, u32[]{:S(2)}, u32[]{:S(2)}) async-start(bf16[16,160,3200]{2,1,0:T(8,128)(2,1)} %tile.2), calls=%async_computation.2 | async-start | bytes 32768000 | tf_op jit(solution)/shard_map/all_to_all | solution.py:19
  1115.3 16.9 %copy-start.17 = (s32[512]{0:T(512)S(1)}, s32[512]{0:T(512)}, u32[]{:S(2)}) copy-start(s32[512]{0:T(512)} %copy-done.16) | copy-start | bytes 6148
  1115.3 39.0 %copy-start.18 = (s32[16]{0:T(128)S(1)}, s32[16]{0:T(128)}, u32[]{:S(2)}) copy-start(s32[16]{0:T(128)} %param.41) | copy-start | bytes 196
  1115.3 39.5 %copy-start.1 = (bf16[640,2560]{1,0:T(8,128)(2,1)S(1)}, bf16[640,2560]{1,0:T(8,128)(2,1)}, u32[]{:S(2)}) copy-start(bf16[640,2560]{1,0:T(8,128)(2,1)} %param.37) | copy-start | bytes 9830404
Sparse Core Ops, SparseCore 0:
  121.9 84.1 all-gather.5
